TPU v7x, 32 devices: a whole 2x2x4 slice. The times are simulated.
32 devices in a mesh: row: 8 (over y, x, core), col: 4 (over z).
Axes of the slice: x: 2, y: 2, z: 4, core: 2. Of those that a mesh axis runs over, the one named last changes fastest.
Arguments:
- density_start: float32 [512, 512], P('row', 'col'), may hold values from -0.5 to 1, as said below
- branches: int32 [6], replicated, may hold values from 0 to 1, as said below
Outputs:
- density: float32 [512, 512], P('row', 'col')
- occupations: float32 [6, 2], replicated
Inputs may be any that keep to these rules, and one draw needn't show every extreme that they name: density_start is symmetric with eigenvalues inside 0 to 1. `branches`: each entry is 0 or 1, and exactly 3 entries are 1.
All inputs are finite; a program needn't handle non-finite values.
Results may differ from a plain program's by a relative error of at most 0.0025.
Values may be sent and summed in bfloat16 or wider, within the bound.
A program may use at most 64 MiB of HBM per device.

v0:
```python
import jax
import jax.numpy as jnp
from jax import lax
from jax.sharding import PartitionSpec as P

ITERS = 6


def taken_in(shard, axis, dim, absorb, state):
    everything = jax.tree.map(lambda a: lax.all_gather(a, axis, axis=dim, tiled=True), shard)
    return absorb(state, everything, jnp.int32(0))


def local_trace(matrix_block, diagonal_mask):
    return jnp.sum(matrix_block * diagonal_mask)


def body(density_start, branches):
    rows_here, cols_here = density_start.shape
    row_first = lax.axis_index("row") * rows_here
    col_first = lax.axis_index("col") * cols_here
    row_ids = row_first + lax.broadcasted_iota(jnp.int32, (rows_here, cols_here), 0)
    col_ids = col_first + lax.broadcasted_iota(jnp.int32, (rows_here, cols_here), 1)
    diagonal_mask = (row_ids == col_ids).astype(jnp.float32)
    size_total = cols_here * lax.axis_size("col")
    density = density_start
    records = []
    for iteration in range(ITERS):
        narrow = density.astype(jnp.bfloat16)
        empty = jnp.zeros((rows_here, cols_here), jnp.float32)
        plain_local = local_trace(density, diagonal_mask)
        row_panel = lax.all_gather(narrow, "col", axis=1, tiled=True)

        def add_rows(accumulated, shard_piece, offset):
            panel_part = lax.dynamic_slice_in_dim(row_panel, offset, shard_piece.shape[0], 1)
            return accumulated + jnp.dot(
                panel_part, shard_piece, preferred_element_type=jnp.float32
            )

        square = taken_in(narrow, "row", 0, add_rows, empty)
        square_local = local_trace(square, diagonal_mask)
        branch_now = branches[iteration]
        records.append(jnp.stack([plain_local, square_local]))
        density = jnp.where(branch_now == 1, 2.0 * density - square, square)
    stacked = jnp.stack(records)
    stacked = lax.psum(stacked, ("row", "col"))
    occupations = stacked / size_total
    return (density, occupations)


def solution(mesh):
    in_specs = (P("row", "col"), P())
    out_specs = (P("row", "col"), P())
    return jax.shard_map(body, mesh=mesh, in_specs=in_specs, out_specs=out_specs, check_vma=False)
```

profile of v0, /device:TPU:0, one launch (start us, length us, event | category | flops | bytes accessed | tf_op | source)
XLA Modules:
  0.0 182.0 jit_solution(16147823306401190443)
XLA Ops:
  0.6 0.0 copy-start
  0.7 1.6 fusion.17
  6.1 0.0 copy-done
  6.1 13.7 %all_gather.36 = bf16[64,512]{1,0:T(8,128)(2,1)S(1)} all-gather(bf16[64,128]{1,0:T(8,128)(2,1)S(1)} %convert_element_type.19), channel_id=1, replica_groups=mesh['row'=8,'col'=4] {'col'}, dimensions={1}, use_global_device_ids=true | all-gather | bytes 81920 | tf_op jit(solution)/shard_map/all_gather | solution.py:32
  19.8 9.2 %all_gather.37 = bf16[512,128]{1,0:T(8,128)(2,1)S(1)} all-gather(bf16[64,128]{1,0:T(8,128)(2,1)S(1)} %convert_element_type.19), channel_id=1, replica_groups=mesh['row'=8,'col'=4] {'row'}, dimensions={0}, use_global_device_ids=true | all-gather | bytes 147456 | tf_op jit(solution)/shard_map/all_gather | solution.py:10
  29.0 0.2 fusion.16
  29.2 12.0 %all_gather.38 = bf16[64,512]{1,0:T(8,128)(2,1)S(1)} all-gather(bf16[64,128]{1,0:T(8,128)(2,1)S(1)} %get-tuple-element.24), channel_id=1, replica_groups=mesh['row'=8,'col'=4] {'col'}, dimensions={1}, use_global_device_ids=true | all-gather | bytes 81920 | tf_op jit(solution)/shard_map/all_gather | solution.py:32
  41.2 9.2 %all_gather.39 = bf16[512,128]{1,0:T(8,128)(2,1)S(1)} all-gather(bf16[64,128]{1,0:T(8,128)(2,1)S(1)} %get-tuple-element.24), channel_id=1, replica_groups=mesh['row'=8,'col'=4] {'row'}, dimensions={0}, use_global_device_ids=true | all-gather | bytes 147456 | tf_op jit(solution)/shard_map/all_gather | solution.py:10
  50.4 0.2 fusion.15
  50.5 12.0 %all_gather.40 = bf16[64,512]{1,0:T(8,128)(2,1)S(1)} all-gather(bf16[64,128]{1,0:T(8,128)(2,1)S(1)} %get-tuple-element.22), channel_id=1, replica_groups=mesh['row'=8,'col'=4] {'col'}, dimensions={1}, use_global_device_ids=true | all-gather | bytes 81920 | tf_op jit(solution)/shard_map/all_gather | solution.py:32
  62.5 8.2 %all_gather.41 = bf16[512,128]{1,0:T(8,128)(2,1)S(1)} all-gather(bf16[64,128]{1,0:T(8,128)(2,1)S(1)} %get-tuple-element.22), channel_id=1, replica_groups=mesh['row'=8,'col'=4] {'row'}, dimensions={0}, use_global_device_ids=true | all-gather | bytes 147456 | tf_op jit(solution)/shard_map/all_gather | solution.py:10
  70.7 0.2 fusion.14
  70.9 12.0 %all_gather.42 = bf16[64,512]{1,0:T(8,128)(2,1)S(1)} all-gather(bf16[64,128]{1,0:T(8,128)(2,1)S(1)} %get-tuple-element.20), channel_id=1, replica_groups=mesh['row'=8,'col'=4] {'col'}, dimensions={1}, use_global_device_ids=true | all-gather | bytes 81920 | tf_op jit(solution)/shard_map/all_gather | solution.py:32
  82.9 9.2 %all_gather.43 = bf16[512,128]{1,0:T(8,128)(2,1)S(1)} all-gather(bf16[64,128]{1,0:T(8,128)(2,1)S(1)} %get-tuple-element.20), channel_id=1, replica_groups=mesh['row'=8,'col'=4] {'row'}, dimensions={0}, use_global_device_ids=true | all-gather | bytes 147456 | tf_op jit(solution)/shard_map/all_gather | solution.py:10
  92.1 0.2 fusion.13
  92.2 12.0 %all_gather.44 = bf16[64,512]{1,0:T(8,128)(2,1)S(1)} all-gather(bf16[64,128]{1,0:T(8,128)(2,1)S(1)} %get-tuple-element.18), channel_id=1, replica_groups=mesh['row'=8,'col'=4] {'col'}, dimensions={1}, use_global_device_ids=true | all-gather | bytes 81920 | tf_op jit(solution)/shard_map/all_gather | solution.py:32
  104.2 8.2 %all_gather.45 = bf16[512,128]{1,0:T(8,128)(2,1)S(1)} all-gather(bf16[64,128]{1,0:T(8,128)(2,1)S(1)} %get-tuple-element.18), channel_id=1, replica_groups=mesh['row'=8,'col'=4] {'row'}, dimensions={0}, use_global_device_ids=true | all-gather | bytes 147456 | tf_op jit(solution)/shard_map/all_gather | solution.py:10
  112.4 0.2 fusion.12
  112.6 12.0 %all_gather.46 = bf16[64,512]{1,0:T(8,128)(2,1)S(1)} all-gather(bf16[64,128]{1,0:T(8,128)(2,1)S(1)} %get-tuple-element.16), channel_id=1, replica_groups=mesh['row'=8,'col'=4] {'col'}, dimensions={1}, use_global_device_ids=true | all-gather | bytes 81920 | tf_op jit(solution)/shard_map/all_gather | solution.py:32
  124.6 9.2 %all_gather.47 = bf16[512,128]{1,0:T(8,128)(2,1)S(1)} all-gather(bf16[64,128]{1,0:T(8,128)(2,1)S(1)} %get-tuple-element.16), channel_id=1, replica_groups=mesh['row'=8,'col'=4] {'row'}, dimensions={0}, use_global_device_ids=true | all-gather | bytes 147456 | tf_op jit(solution)/shard_map/all_gather | solution.py:10
  133.8 1.5 fusion.10
  135.2 1.3 maximum_bitcast_fusion.5
  136.5 0.1 copy.10
  136.6 1.3 maximum_bitcast_fusion.4
  138.0 0.1 copy.9
  138.1 1.3 maximum_bitcast_fusion.3
  139.4 0.1 copy.8
  139.4 1.3 maximum_bitcast_fusion.2
  140.8 0.1 copy.7
  140.9 1.3 maximum_bitcast_fusion.1
  142.2 0.1 copy.6
  142.3 1.3 maximum_bitcast_fusion
  143.6 0.1 copy.5
  143.7 0.1 stack.99
  143.8 37.7 %psum.7 = f32[6,2]{0,1:T(2,128)S(1)} all-reduce(f32[6,2]{0,1:T(2,128)S(1)} %stack.99), channel_id=1, replica_groups=mesh['row'=8,'col'=4] {'row','col'}, use_global_device_ids=true, to_apply=%region_12.13 | all-reduce | flops 12 | bytes 96 | tf_op jit(solution)/shard_map/psum | solution.py:46
  181.5 0.6 broadcast_multiply_fusion
  (3 shorter events, 0.0 us)
Async XLA Ops:
  0.6 5.5 %copy-start = (f32[64,128]{1,0:T(8,128)S(1)}, f32[64,128]{1,0:T(8,128)}, u32[]{:S(2)}) copy-start(f32[64,128]{1,0:T(8,128)} %param.2) | copy-start | bytes 98308
where the time goes:
time: 183 us; the launch traced here: 182 us
  blocking collectives  165 us (90%)
  other arithmetic  8.46 us (5%)
  between operations  4.56 us (2%)
  matrix products  2.26 us (1%)
  local copies, waits for them, and re-layouts  2.23 us (1%)
    all_gather x6, blocking collectives, body(): row_panel = lax.all_gather(narrow, 'col', axis=1, tiled=True)  73.7 us
    all_gather x6, blocking collectives, taken_in(): lax.all_gather(a, axis, axis=dim, tiled=True)  53.2 us
    psum x1, blocking collectives, body(): stacked = lax.psum(stacked, ('row', 'col'))  37.7 us
    another operation x6, other arithmetic, body(): stacked = jnp.stack(records)  7.88 us

commit v1 on v0

--- a/solution.py
+++ b/solution.py
@@ -29,7 +29,14 @@
         narrow = density.astype(jnp.bfloat16)
         empty = jnp.zeros((rows_here, cols_here), jnp.float32)
         plain_local = local_trace(density, diagonal_mask)
-        row_panel = lax.all_gather(narrow, "col", axis=1, tiled=True)
+        ring = [narrow]
+        for hop in range(3):
+            ring.append(lax.ppermute(ring[-1], "col", [(dev, (dev + 1) % 4) for dev in range(4)]))
+        row_panel = jnp.roll(
+            jnp.concatenate(ring[::-1], axis=1),
+            (lax.axis_index("col") + 1) * ring[0].shape[1],
+            axis=1,
+        )
 
         def add_rows(accumulated, shard_piece, offset):
             panel_part = lax.dynamic_slice_in_dim(row_panel, offset, shard_piece.shape[0], 1)

time: 183 us -> 174 us (0.951)
  blocking collectives: 165 us -> 92.5 us
  waiting for transfers between devices: 0 us -> 60 us
  starting transfers between devices: 0 us -> 3.38 us
  other arithmetic: 8.46 us -> 10.6 us
    all_gather x6 -> x0, blocking collectives: 73.7 us -> none  [body(): row_panel = lax.all_gather(narrow, 'col', axis=1, tiled=True)]
    ppermute x0 -> x18, waiting for transfers between devices: none -> 60 us  [body(): lax.ppermute(ring[-1], 'col', [(dev, (dev + 1) % 4) for dev in range(4)])]
    ppermute x0 -> x18, starting transfers between devices: none -> 3.38 us  [body(): lax.ppermute(ring[-1], 'col', [(dev, (dev + 1) % 4) for dev in range(4)])]
  transfers between devices with their start and end apart: 0 -> 18, of which waited for: 0 -> 12; matrix products, arithmetic and copies ran while one was open for 0% -> 0% of each run, Pallas kernels for 0% -> 0%
where the time goes in v1:
time: 174 us
  blocking collectives  92.5 us (53%)
  waiting for transfers between devices  60 us (34%)
  other arithmetic  10.6 us (6%)
  between operations  4.61 us (3%)
  starting transfers between devices  3.38 us (2%)
    ppermute x18, waiting for transfers between devices, body(): lax.ppermute(ring[-1], 'col', [(dev, (dev + 1) % 4) for dev in range(4)])  60 us
    all_gather x6, blocking collectives, taken_in(): lax.all_gather(a, axis, axis=dim, tiled=True)  53.4 us
    psum x1, blocking collectives, body(): stacked = lax.psum(stacked, ('row', 'col'))  39.1 us
    another operation x6, other arithmetic, body(): stacked = jnp.stack(records)  7.88 us
  transfers between devices with their start and end apart: 18, of which 12 were waited for; matrix products, arithmetic and copies ran while one was open for 0% of the time, Pallas kernels for 0%

profile of v1, /device:TPU:0, one launch (start us, length us, event | category | flops | bytes accessed | tf_op | source)
XLA Modules:
  0.0 173.7 jit_solution(11636717020355028321)
XLA Ops:
  0.6 0.8 convert_element_type.19
  1.4 3.1 %collective-permute-start = (bf16[64,128]{1,0:T(8,128)(2,1)S(1)}, bf16[64,128]{1,0:T(8,128)(2,1)S(1)}, u32[]{:S(2)}, u32[]{:S(2)}) collective-permute-start(bf16[64,128]{1,0:T(8,128)(2,1)S(1)} %convert_element_type.19), channel_id=1, source_target_pairs={{0,1},{1,2},{2,3},{3,0},{4,5},{5,6},{6,7},{7,4},{8,9},{9,10},{10,1... | collective-permute-start | bytes 49160 | tf_op jit(solution)/shard_map/ppermute | solution.py:34
  4.5 3.7 %collective-permute-done = bf16[64,128]{1,0:T(8,128)(2,1)S(1)} collective-permute-done((bf16[64,128]{1,0:T(8,128)(2,1)S(1)}, bf16[64,128]{1,0:T(8,128)(2,1)S(1)}, u32[]{:S(2)}, u32[]{:S(2)}) %collective-permute-start) | collective-permute-done | bytes 16416 | tf_op jit(solution)/shard_map/ppermute | solution.py:34
  8.2 0.7 fusion.89
  9.5 4.2 %collective-permute-done.1 = bf16[64,128]{1,0:T(8,128)(2,1)S(1)} collective-permute-done((bf16[64,128]{1,0:T(8,128)(2,1)S(1)}, bf16[64,128]{1,0:T(8,128)(2,1)S(1)}, u32[]{:S(2)}, u32[]{:S(2)}) %collective-permute-start.1) | collective-permute-done | bytes 16416 | tf_op jit(solution)/shard_map/ppermute | solution.py:34
  13.7 9.4 %all_gather.18 = bf16[512,128]{1,0:T(8,128)(2,1)S(1)} all-gather(bf16[64,128]{1,0:T(8,128)(2,1)S(1)} %convert_element_type.19), channel_id=1, replica_groups=mesh['row'=8,'col'=4] {'row'}, dimensions={0}, use_global_device_ids=true | all-gather | bytes 147456 | tf_op jit(solution)/shard_map/all_gather | solution.py:10
  23.2 0.2 fusion.88
  23.4 0.1 collective-permute-start.3
  23.5 5.5 %collective-permute-done.3 = bf16[64,128]{1,0:T(8,128)(2,1)S(1)} collective-permute-done((bf16[64,128]{1,0:T(8,128)(2,1)S(1)}, bf16[64,128]{1,0:T(8,128)(2,1)S(1)}, u32[]{:S(2)}, u32[]{:S(2)}) %collective-permute-start.3) | collective-permute-done | bytes 16416 | tf_op jit(solution)/shard_map/ppermute | solution.py:34
  29.6 4.9 %collective-permute-done.4 = bf16[64,128]{1,0:T(8,128)(2,1)S(1)} collective-permute-done((bf16[64,128]{1,0:T(8,128)(2,1)S(1)}, bf16[64,128]{1,0:T(8,128)(2,1)S(1)}, u32[]{:S(2)}, u32[]{:S(2)}) %collective-permute-start.4) | collective-permute-done | bytes 16416 | tf_op jit(solution)/shard_map/ppermute | solution.py:34
  34.5 9.2 %all_gather.19 = bf16[512,128]{1,0:T(8,128)(2,1)S(1)} all-gather(bf16[64,128]{1,0:T(8,128)(2,1)S(1)} %get-tuple-element.25), channel_id=1, replica_groups=mesh['row'=8,'col'=4] {'row'}, dimensions={0}, use_global_device_ids=true | all-gather | bytes 147456 | tf_op jit(solution)/shard_map/all_gather | solution.py:10
  43.7 0.2 fusion.87
  43.9 0.1 collective-permute-start.6
  44.0 5.5 %collective-permute-done.6 = bf16[64,128]{1,0:T(8,128)(2,1)S(1)} collective-permute-done((bf16[64,128]{1,0:T(8,128)(2,1)S(1)}, bf16[64,128]{1,0:T(8,128)(2,1)S(1)}, u32[]{:S(2)}, u32[]{:S(2)}) %collective-permute-start.6) | collective-permute-done | bytes 16416 | tf_op jit(solution)/shard_map/ppermute | solution.py:34
  50.2 4.9 %collective-permute-done.7 = bf16[64,128]{1,0:T(8,128)(2,1)S(1)} collective-permute-done((bf16[64,128]{1,0:T(8,128)(2,1)S(1)}, bf16[64,128]{1,0:T(8,128)(2,1)S(1)}, u32[]{:S(2)}, u32[]{:S(2)}) %collective-permute-start.7) | collective-permute-done | bytes 16416 | tf_op jit(solution)/shard_map/ppermute | solution.py:34
  55.1 8.2 %all_gather.20 = bf16[512,128]{1,0:T(8,128)(2,1)S(1)} all-gather(bf16[64,128]{1,0:T(8,128)(2,1)S(1)} %get-tuple-element.23), channel_id=1, replica_groups=mesh['row'=8,'col'=4] {'row'}, dimensions={0}, use_global_device_ids=true | all-gather | bytes 147456 | tf_op jit(solution)/shard_map/all_gather | solution.py:10
  63.3 0.2 fusion.86
  63.5 0.1 collective-permute-start.9
  63.6 5.5 %collective-permute-done.9 = bf16[64,128]{1,0:T(8,128)(2,1)S(1)} collective-permute-done((bf16[64,128]{1,0:T(8,128)(2,1)S(1)}, bf16[64,128]{1,0:T(8,128)(2,1)S(1)}, u32[]{:S(2)}, u32[]{:S(2)}) %collective-permute-start.9) | collective-permute-done | bytes 16416 | tf_op jit(solution)/shard_map/ppermute | solution.py:34
  69.8 4.8 %collective-permute-done.10 = bf16[64,128]{1,0:T(8,128)(2,1)S(1)} collective-permute-done((bf16[64,128]{1,0:T(8,128)(2,1)S(1)}, bf16[64,128]{1,0:T(8,128)(2,1)S(1)}, u32[]{:S(2)}, u32[]{:S(2)}) %collective-permute-start.10) | collective-permute-done | bytes 16416 | tf_op jit(solution)/shard_map/ppermute | solution.py:34
  74.7 9.2 %all_gather.21 = bf16[512,128]{1,0:T(8,128)(2,1)S(1)} all-gather(bf16[64,128]{1,0:T(8,128)(2,1)S(1)} %get-tuple-element.21), channel_id=1, replica_groups=mesh['row'=8,'col'=4] {'row'}, dimensions={0}, use_global_device_ids=true | all-gather | bytes 147456 | tf_op jit(solution)/shard_map/all_gather | solution.py:10
  83.8 0.2 fusion.85
  84.1 0.1 collective-permute-start.12
  84.1 5.5 %collective-permute-done.12 = bf16[64,128]{1,0:T(8,128)(2,1)S(1)} collective-permute-done((bf16[64,128]{1,0:T(8,128)(2,1)S(1)}, bf16[64,128]{1,0:T(8,128)(2,1)S(1)}, u32[]{:S(2)}, u32[]{:S(2)}) %collective-permute-start.12) | collective-permute-done | bytes 16416 | tf_op jit(solution)/shard_map/ppermute | solution.py:34
  90.2 5.0 %collective-permute-done.13 = bf16[64,128]{1,0:T(8,128)(2,1)S(1)} collective-permute-done((bf16[64,128]{1,0:T(8,128)(2,1)S(1)}, bf16[64,128]{1,0:T(8,128)(2,1)S(1)}, u32[]{:S(2)}, u32[]{:S(2)}) %collective-permute-start.13) | collective-permute-done | bytes 16416 | tf_op jit(solution)/shard_map/ppermute | solution.py:34
  95.2 8.2 %all_gather.22 = bf16[512,128]{1,0:T(8,128)(2,1)S(1)} all-gather(bf16[64,128]{1,0:T(8,128)(2,1)S(1)} %get-tuple-element.19), channel_id=1, replica_groups=mesh['row'=8,'col'=4] {'row'}, dimensions={0}, use_global_device_ids=true | all-gather | bytes 147456 | tf_op jit(solution)/shard_map/all_gather | solution.py:10
  103.4 0.2 fusion.84
  103.6 0.1 collective-permute-start.15
  103.7 5.5 %collective-permute-done.15 = bf16[64,128]{1,0:T(8,128)(2,1)S(1)} collective-permute-done((bf16[64,128]{1,0:T(8,128)(2,1)S(1)}, bf16[64,128]{1,0:T(8,128)(2,1)S(1)}, u32[]{:S(2)}, u32[]{:S(2)}) %collective-permute-start.15) | collective-permute-done | bytes 16416 | tf_op jit(solution)/shard_map/ppermute | solution.py:34
  109.9 4.9 %collective-permute-done.16 = bf16[64,128]{1,0:T(8,128)(2,1)S(1)} collective-permute-done((bf16[64,128]{1,0:T(8,128)(2,1)S(1)}, bf16[64,128]{1,0:T(8,128)(2,1)S(1)}, u32[]{:S(2)}, u32[]{:S(2)}) %collective-permute-start.16) | collective-permute-done | bytes 16416 | tf_op jit(solution)/shard_map/ppermute | solution.py:34
  114.8 9.2 %all_gather.23 = bf16[512,128]{1,0:T(8,128)(2,1)S(1)} all-gather(bf16[64,128]{1,0:T(8,128)(2,1)S(1)} %get-tuple-element.17), channel_id=1, replica_groups=mesh['row'=8,'col'=4] {'row'}, dimensions={0}, use_global_device_ids=true | all-gather | bytes 147456 | tf_op jit(solution)/shard_map/all_gather | solution.py:10
  124.0 0.2 fusion.4
  124.2 1.3 fusion.70
  125.5 1.3 maximum_bitcast_fusion.5
  126.8 0.1 copy.10
  126.9 1.3 maximum_bitcast_fusion.4
  128.2 0.1 copy.9
  128.3 1.3 maximum_bitcast_fusion.3
  129.6 0.1 copy.8
  129.7 1.3 maximum_bitcast_fusion.2
  131.0 0.1 copy.7
  131.1 1.3 maximum_bitcast_fusion.1
  132.5 0.1 copy.6
  132.5 1.3 maximum_bitcast_fusion
  133.9 0.1 copy.5
  134.0 0.1 stack.99
  134.1 39.1 %psum.7 = f32[6,2]{0,1:T(2,128)S(1)} all-reduce(f32[6,2]{0,1:T(2,128)S(1)} %stack.99), channel_id=1, replica_groups=mesh['row'=8,'col'=4] {'row','col'}, use_global_device_ids=true, to_apply=%region_12.14 | all-reduce | flops 12 | bytes 96 | tf_op jit(solution)/shard_map/psum | solution.py:53
  173.1 0.6 broadcast_multiply_fusion
  (24 shorter events, 0.1 us)
Async XLA Ops:
  0.6 7.6 %copy-start.1 = (s32[6]{0:T(128)S(1)}, s32[6]{0:T(128)}, u32[]{:S(2)}) copy-start(s32[6]{0:T(128)} %param.5) | copy-start | bytes 76
  1.4 6.8 %collective-permute-start = (bf16[64,128]{1,0:T(8,128)(2,1)S(1)}, bf16[64,128]{1,0:T(8,128)(2,1)S(1)}, u32[]{:S(2)}, u32[]{:S(2)}) collective-permute-start(bf16[64,128]{1,0:T(8,128)(2,1)S(1)} %convert_element_type.19), channel_id=1, source_target_pairs={{0,1},{1,2},{2,3},{3,0},{4,5},{5,6},{6,7},{7,4},{8,9},{9,10},{10,1... | collective-permute-start | bytes 49160 | tf_op jit(solution)/shard_map/ppermute | solution.py:34
  8.2 5.5 %collective-permute-start.1 = (bf16[64,128]{1,0:T(8,128)(2,1)S(1)}, bf16[64,128]{1,0:T(8,128)(2,1)S(1)}, u32[]{:S(2)}, u32[]{:S(2)}) collective-permute-start(bf16[64,128]{1,0:T(8,128)(2,1)S(1)} %collective-permute-done), channel_id=1, source_target_pairs={{0,1},{1,2},{2,3},{3,0},{4,5},{5,6},{6,7},{7,4},{8,9},{9,10},{10,1... | collective-permute-start | bytes 49160 | tf_op jit(solution)/shard_map/ppermute | solution.py:34
  9.5 13.6 %copy-start = (f32[64,128]{1,0:T(8,128)S(1)}, f32[64,128]{1,0:T(8,128)}, u32[]{:S(2)}) copy-start(f32[64,128]{1,0:T(8,128)} %param.4) | copy-start | bytes 98308
  13.7 9.4 %collective-permute-start.2 = (bf16[64,128]{1,0:T(8,128)(2,1)S(1)}, bf16[64,128]{1,0:T(8,128)(2,1)S(1)}, u32[]{:S(2)}, u32[]{:S(2)}) collective-permute-start(bf16[64,128]{1,0:T(8,128)(2,1)S(1)} %collective-permute-done.1), channel_id=1, source_target_pairs={{0,1},{1,2},{2,3},{3,0},{4,5},{5,6},{6,7},{7,4},{8,9},{9,10},{10,1... | collective-permute-start | bytes 49160 | tf_op jit(solution)/shard_map/ppermute | solution.py:34
  23.4 5.6 %collective-permute-start.3 = (bf16[64,128]{1,0:T(8,128)(2,1)S(1)}, bf16[64,128]{1,0:T(8,128)(2,1)S(1)}, u32[]{:S(2)}, u32[]{:S(2)}) collective-permute-start(bf16[64,128]{1,0:T(8,128)(2,1)S(1)} %get-tuple-element.25), channel_id=1, source_target_pairs={{0,1},{1,2},{2,3},{3,0},{4,5},{5,6},{6,7},{7,4},{8,9},{9,10},{10,1... | collective-permute-start | bytes 49160 | tf_op jit(solution)/shard_map/ppermute | solution.py:34
  29.0 5.5 %collective-permute-start.4 = (bf16[64,128]{1,0:T(8,128)(2,1)S(1)}, bf16[64,128]{1,0:T(8,128)(2,1)S(1)}, u32[]{:S(2)}, u32[]{:S(2)}) collective-permute-start(bf16[64,128]{1,0:T(8,128)(2,1)S(1)} %collective-permute-done.3), channel_id=1, source_target_pairs={{0,1},{1,2},{2,3},{3,0},{4,5},{5,6},{6,7},{7,4},{8,9},{9,10},{10,1... | collective-permute-start | bytes 49160 | tf_op jit(solution)/shard_map/ppermute | solution.py:34
  34.5 9.2 %collective-permute-start.5 = (bf16[64,128]{1,0:T(8,128)(2,1)S(1)}, bf16[64,128]{1,0:T(8,128)(2,1)S(1)}, u32[]{:S(2)}, u32[]{:S(2)}) collective-permute-start(bf16[64,128]{1,0:T(8,128)(2,1)S(1)} %collective-permute-done.4), channel_id=1, source_target_pairs={{0,1},{1,2},{2,3},{3,0},{4,5},{5,6},{6,7},{7,4},{8,9},{9,10},{10,1... | collective-permute-start | bytes 49160 | tf_op jit(solution)/shard_map/ppermute | solution.py:34
  43.9 5.6 %collective-permute-start.6 = (bf16[64,128]{1,0:T(8,128)(2,1)S(1)}, bf16[64,128]{1,0:T(8,128)(2,1)S(1)}, u32[]{:S(2)}, u32[]{:S(2)}) collective-permute-start(bf16[64,128]{1,0:T(8,128)(2,1)S(1)} %get-tuple-element.23), channel_id=1, source_target_pairs={{0,1},{1,2},{2,3},{3,0},{4,5},{5,6},{6,7},{7,4},{8,9},{9,10},{10,1... | collective-permute-start | bytes 49160 | tf_op jit(solution)/shard_map/ppermute | solution.py:34
  49.5 5.5 %collective-permute-start.7 = (bf16[64,128]{1,0:T(8,128)(2,1)S(1)}, bf16[64,128]{1,0:T(8,128)(2,1)S(1)}, u32[]{:S(2)}, u32[]{:S(2)}) collective-permute-start(bf16[64,128]{1,0:T(8,128)(2,1)S(1)} %collective-permute-done.6), channel_id=1, source_target_pairs={{0,1},{1,2},{2,3},{3,0},{4,5},{5,6},{6,7},{7,4},{8,9},{9,10},{10,1... | collective-permute-start | bytes 49160 | tf_op jit(solution)/shard_map/ppermute | solution.py:34
  55.1 8.2 %collective-permute-start.8 = (bf16[64,128]{1,0:T(8,128)(2,1)S(1)}, bf16[64,128]{1,0:T(8,128)(2,1)S(1)}, u32[]{:S(2)}, u32[]{:S(2)}) collective-permute-start(bf16[64,128]{1,0:T(8,128)(2,1)S(1)} %collective-permute-done.7), channel_id=1, source_target_pairs={{0,1},{1,2},{2,3},{3,0},{4,5},{5,6},{6,7},{7,4},{8,9},{9,10},{10,1... | collective-permute-start | bytes 49160 | tf_op jit(solution)/shard_map/ppermute | solution.py:34
  63.5 5.6 %collective-permute-start.9 = (bf16[64,128]{1,0:T(8,128)(2,1)S(1)}, bf16[64,128]{1,0:T(8,128)(2,1)S(1)}, u32[]{:S(2)}, u32[]{:S(2)}) collective-permute-start(bf16[64,128]{1,0:T(8,128)(2,1)S(1)} %get-tuple-element.21), channel_id=1, source_target_pairs={{0,1},{1,2},{2,3},{3,0},{4,5},{5,6},{6,7},{7,4},{8,9},{9,10},{10,1... | collective-permute-start | bytes 49160 | tf_op jit(solution)/shard_map/ppermute | solution.py:34
  69.1 5.5 %collective-permute-start.10 = (bf16[64,128]{1,0:T(8,128)(2,1)S(1)}, bf16[64,128]{1,0:T(8,128)(2,1)S(1)}, u32[]{:S(2)}, u32[]{:S(2)}) collective-permute-start(bf16[64,128]{1,0:T(8,128)(2,1)S(1)} %collective-permute-done.9), channel_id=1, source_target_pairs={{0,1},{1,2},{2,3},{3,0},{4,5},{5,6},{6,7},{7,4},{8,9},{9,10},{10,1... | collective-permute-start | bytes 49160 | tf_op jit(solution)/shard_map/ppermute | solution.py:34
  74.7 9.2 %collective-permute-start.11 = (bf16[64,128]{1,0:T(8,128)(2,1)S(1)}, bf16[64,128]{1,0:T(8,128)(2,1)S(1)}, u32[]{:S(2)}, u32[]{:S(2)}) collective-permute-start(bf16[64,128]{1,0:T(8,128)(2,1)S(1)} %collective-permute-done.10), channel_id=1, source_target_pairs={{0,1},{1,2},{2,3},{3,0},{4,5},{5,6},{6,7},{7,4},{8,9},{9,10},{10,1... | collective-permute-start | bytes 49160 | tf_op jit(solution)/shard_map/ppermute | solution.py:34
  84.1 5.6 %collective-permute-start.12 = (bf16[64,128]{1,0:T(8,128)(2,1)S(1)}, bf16[64,128]{1,0:T(8,128)(2,1)S(1)}, u32[]{:S(2)}, u32[]{:S(2)}) collective-permute-start(bf16[64,128]{1,0:T(8,128)(2,1)S(1)} %get-tuple-element.19), channel_id=1, source_target_pairs={{0,1},{1,2},{2,3},{3,0},{4,5},{5,6},{6,7},{7,4},{8,9},{9,10},{10,1... | collective-permute-start | bytes 49160 | tf_op jit(solution)/shard_map/ppermute | solution.py:34
  89.7 5.5 %collective-permute-start.13 = (bf16[64,128]{1,0:T(8,128)(2,1)S(1)}, bf16[64,128]{1,0:T(8,128)(2,1)S(1)}, u32[]{:S(2)}, u32[]{:S(2)}) collective-permute-start(bf16[64,128]{1,0:T(8,128)(2,1)S(1)} %collective-permute-done.12), channel_id=1, source_target_pairs={{0,1},{1,2},{2,3},{3,0},{4,5},{5,6},{6,7},{7,4},{8,9},{9,10},{10,1... | collective-permute-start | bytes 49160 | tf_op jit(solution)/shard_map/ppermute | solution.py:34
  95.2 8.2 %collective-permute-start.14 = (bf16[64,128]{1,0:T(8,128)(2,1)S(1)}, bf16[64,128]{1,0:T(8,128)(2,1)S(1)}, u32[]{:S(2)}, u32[]{:S(2)}) collective-permute-start(bf16[64,128]{1,0:T(8,128)(2,1)S(1)} %collective-permute-done.13), channel_id=1, source_target_pairs={{0,1},{1,2},{2,3},{3,0},{4,5},{5,6},{6,7},{7,4},{8,9},{9,10},{10,1... | collective-permute-start | bytes 49160 | tf_op jit(solution)/shard_map/ppermute | solution.py:34
  103.6 5.6 %collective-permute-start.15 = (bf16[64,128]{1,0:T(8,128)(2,1)S(1)}, bf16[64,128]{1,0:T(8,128)(2,1)S(1)}, u32[]{:S(2)}, u32[]{:S(2)}) collective-permute-start(bf16[64,128]{1,0:T(8,128)(2,1)S(1)} %get-tuple-element.17), channel_id=1, source_target_pairs={{0,1},{1,2},{2,3},{3,0},{4,5},{5,6},{6,7},{7,4},{8,9},{9,10},{10,1... | collective-permute-start | bytes 49160 | tf_op jit(solution)/shard_map/ppermute | solution.py:34
  109.2 5.5 %collective-permute-start.16 = (bf16[64,128]{1,0:T(8,128)(2,1)S(1)}, bf16[64,128]{1,0:T(8,128)(2,1)S(1)}, u32[]{:S(2)}, u32[]{:S(2)}) collective-permute-start(bf16[64,128]{1,0:T(8,128)(2,1)S(1)} %collective-permute-done.15), channel_id=1, source_target_pairs={{0,1},{1,2},{2,3},{3,0},{4,5},{5,6},{6,7},{7,4},{8,9},{9,10},{10,1... | collective-permute-start | bytes 49160 | tf_op jit(solution)/shard_map/ppermute | solution.py:34
  114.8 9.2 %collective-permute-start.17 = (bf16[64,128]{1,0:T(8,128)(2,1)S(1)}, bf16[64,128]{1,0:T(8,128)(2,1)S(1)}, u32[]{:S(2)}, u32[]{:S(2)}) collective-permute-start(bf16[64,128]{1,0:T(8,128)(2,1)S(1)} %collective-permute-done.16), channel_id=1, source_target_pairs={{0,1},{1,2},{2,3},{3,0},{4,5},{5,6},{6,7},{7,4},{8,9},{9,10},{10,1... | collective-permute-start | bytes 49160 | tf_op jit(solution)/shard_map/ppermute | solution.py:34
